TPU v7x, 256 devices: a whole 4x4x8 slice. The times are simulated.
256 devices in a mesh: head: 2 (over core), blk: 32 (over z, x), rep: 4 (over y).
Axes of the slice: x: 4, y: 4, z: 8, core: 2. Of those that a mesh axis runs over, the one named last changes fastest.
Arguments:
- queries: bfloat16 [16384, 768], P(('blk', 'rep'), 'head'), may hold values from -400 to 400
- keys: bfloat16 [16384, 256], P(('blk', 'rep'), 'head'), may hold values from -6 to 6
- values: bfloat16 [16384, 256], P(('blk', 'rep'), 'head'), may hold values from -18 to 18
- stretch_order: int32 [128], replicated, may hold values from 0 to 127, each once
- out_weight: bfloat16 [768, 3072], P('head'), may hold values from -0.21875 to 0.21875
Outputs:
- mixed_rows: bfloat16 [16384, 3072], P(('blk', 'rep'), 'head')
- log_sum_exp: float32 [6, 16384], P('head', ('blk', 'rep'))
Inputs may be any that keep to these rules, and one draw needn't show every extreme that they name: `stretch_order`: each stretch number appears once.
All inputs are finite; a program needn't handle non-finite values.
Results may differ from a plain program's by a relative error of at most 0.02.
Values may be sent and summed in bfloat16 or wider, within the bound.
A program may use at most 128 MiB of HBM per device.

v0:
```python
import math

import jax
import jax.numpy as jnp
from jax import lax
from jax.sharding import Mesh
from jax.sharding import PartitionSpec as P

GROUP = 3
DH = 128
BLK = ("blk_0", "blk_1")
BLK_REP = ("blk_0", "blk_1", "rep")


NEG_FILL = -1e30
BLOCK_ROWS = 512


def whole_of(x, axes, dim):
    for axis in reversed(axes):
        x = lax.all_gather(x, axis, axis=dim, tiled=True)
    return x


def side_by_side(arrays, axis, dim, along):
    ends, at = ([], 0)
    for a in arrays[:-1]:
        at += a.shape[along]
        ends.append(at)
    both = jnp.concatenate(arrays, axis=along)
    return tuple(jnp.split(lax.all_gather(both, axis, axis=dim, tiled=True), ends, axis=along))


def side_by_side_2(arrays, axis, split_dim, concat_dim, along):
    widths = [math.prod(a.shape[along:]) for a in arrays]
    both = jnp.concatenate(
        [a.reshape(*a.shape[:along], w) for a, w in zip(arrays, widths)], axis=along
    )
    whole = lax.all_to_all(both, axis, split_axis=split_dim, concat_axis=concat_dim, tiled=True)
    pieces = jnp.split(whole, [sum(widths[:k]) for k in range(1, len(widths))], axis=along)
    return tuple(
        (b.reshape(*whole.shape[:along], *a.shape[along:]) for a, b in zip(arrays, pieces))
    )


def cut_along(x, dim, devices):
    shape = x.shape
    pieces = x.reshape(*shape[:dim], devices, shape[dim] // devices, *shape[dim + 1 :])
    return jnp.moveaxis(pieces, dim, 0)


def summed_on_arrival(x, axis, dim):
    devices = lax.axis_size(axis)
    pieces = lax.all_to_all(cut_along(x, dim, devices), axis, 0, 0, tiled=True)
    return jnp.sum(pieces.astype(jnp.float32), axis=0)


def stretch_starts(stretch_order, block_ids, tok_rows):
    stretch_ids = jnp.arange(stretch_order.shape[0], dtype=jnp.int32)
    onehot = (block_ids[:, None] == stretch_ids[None, :]).astype(jnp.int32)
    return jnp.sum(onehot * stretch_order[None, :], axis=1) * tok_rows


def attend_piece(running, pieces, query_heads, query_pos, key_block_of, stretch_order, tok_rows):
    key_rows, value_rows = pieces
    length = key_rows.shape[0]
    kv_heads = query_heads.shape[0]
    head_dim = query_heads.shape[2]
    key_table = key_rows.reshape(length, kv_heads, head_dim)
    value_table = value_rows.reshape(length, kv_heads, head_dim)
    step_rows = math.gcd(length, BLOCK_ROWS)
    latest = jnp.max(query_pos)
    factor = head_dim ** (-0.5)

    def one_block(block_index, current):
        offset = block_index * step_rows
        rows_whole = offset + jnp.arange(step_rows, dtype=jnp.int32)
        key_pos = (
            stretch_starts(stretch_order, key_block_of(rows_whole // tok_rows), tok_rows)
            + rows_whole % tok_rows
        )

        def update(previous):
            row_max, totals, numerator = previous
            scores = (
                jnp.einsum(
                    "hqd,khd->hqk", query_heads, key_table, preferred_element_type=jnp.float32
                )
                * factor
            )
            allowed = key_pos[None, None, :] <= query_pos[None, :, None]
            scores = jnp.where(allowed, scores, NEG_FILL)
            new_max = jnp.maximum(row_max, jnp.max(scores, axis=2))
            rescale = jnp.exp(row_max - new_max)
            weights = jnp.exp(scores - new_max[:, :, None])
            totals = totals * rescale + jnp.sum(weights, axis=2)
            numerator = numerator * rescale[:, :, None] + jnp.einsum(
                "hqk,khd->hqd",
                weights.astype(jnp.bfloat16),
                value_table,
                preferred_element_type=jnp.float32,
            )
            return (new_max, totals, numerator)

        def keep_all(previous):
            return previous

        return lax.cond(jnp.min(key_pos) <= latest, update, keep_all, current)

    return lax.fori_loop(0, length // step_rows, one_block, running)


def body(queries, keys, values, stretch_order, out_weight):
    tok_rows = queries.shape[0]
    head_dim = DH
    group_size = GROUP
    kv_heads = keys.shape[1] // head_dim
    blk_rank = lax.axis_index(BLK)
    rep_rank = lax.axis_index("rep")
    spans = lax.axis_size(BLK)
    span_len = lax.axis_size("rep")
    gathered_queries = whole_of(queries, BLK, 0)
    query_blocks = jnp.arange(spans * tok_rows, dtype=jnp.int32) // tok_rows * span_len + rep_rank

    def key_block_of(cycle_block):
        return blk_rank * span_len + cycle_block

    count_rows = gathered_queries.shape[0]
    query_pos = (
        stretch_starts(stretch_order, query_blocks, tok_rows)
        + jnp.arange(count_rows, dtype=jnp.int32) % tok_rows
    )
    query_heads = gathered_queries.reshape(count_rows, kv_heads, group_size, head_dim).transpose(
        1, 2, 0, 3
    )
    query_heads = query_heads.reshape(kv_heads, group_size * count_rows, head_dim)
    query_pos_all = jnp.tile(query_pos, group_size)
    initial = (
        jnp.full((kv_heads, group_size * count_rows), NEG_FILL, jnp.float32),
        jnp.zeros((kv_heads, group_size * count_rows), jnp.float32),
        jnp.zeros((kv_heads, group_size * count_rows, head_dim), jnp.float32),
    )
    row_max, totals, numerator = attend_piece(
        initial,
        side_by_side((keys, values), "rep", 0, 1),
        query_heads,
        query_pos_all,
        key_block_of,
        stretch_order,
        tok_rows,
    )
    exchanged = side_by_side_2(
        (
            row_max.reshape(kv_heads, group_size, spans, tok_rows),
            totals.reshape(kv_heads, group_size, spans, tok_rows),
            numerator.reshape(kv_heads, group_size, spans, tok_rows, head_dim),
        ),
        BLK,
        2,
        2,
        4,
    )
    own_max = jnp.max(exchanged[0], axis=2)
    shrink = jnp.exp(exchanged[0] - own_max[:, :, None, :])
    own_totals = jnp.sum(exchanged[1] * shrink, axis=2)
    own_numer = jnp.sum(exchanged[2] * shrink[..., None], axis=2)
    attended = (own_numer / own_totals[..., None]).astype(jnp.bfloat16)
    log_sum = (own_max + jnp.log(own_totals)).reshape(kv_heads * group_size, tok_rows)
    attended_rows = attended.transpose(2, 0, 1, 3).reshape(
        tok_rows, kv_heads * group_size * head_dim
    )
    partial_value = jnp.dot(attended_rows, out_weight, preferred_element_type=jnp.float32)
    mixed_rows = summed_on_arrival(partial_value.astype(jnp.bfloat16), "head", 1).astype(
        jnp.bfloat16
    )
    return (mixed_rows, log_sum)


def solution(mesh):
    split = Mesh(
        mesh.devices.reshape(mesh.shape["head"], 8, 4, mesh.shape["rep"]),
        ("head", "blk_0", "blk_1", "rep"),
    )
    in_specs = (P(BLK_REP, "head"), P(BLK_REP, "head"), P(BLK_REP, "head"), P(), P("head", None))
    out_specs = (P(BLK_REP, "head"), P("head", BLK_REP))
    return jax.shard_map(body, mesh=split, in_specs=in_specs, out_specs=out_specs, check_vma=False)
```

profile of v0, /device:TPU:1, one launch (start us, length us, event | category | flops | bytes accessed | tf_op | source)
XLA Modules:
  0.0 305.0 jit_solution(12356893755944874380)
XLA Ops:
  7.2 0.0 copy-start
  7.2 0.0 copy-start.2
  7.2 0.0 copy-start.1
  7.2 0.0 all-gather.2.cloned.1.call-start
  7.2 1.2 copy.36
  8.4 12.3 %all_gather.9 = bf16[512,384]{0,1:T(8,128)(2,1)} all-gather(bf16[128,384]{0,1:T(8,128)(2,1)S(1)} %copy.36), channel_id=1, replica_groups=mesh['head'=2,'blk_0'=8,'blk_1'=4,'rep'=4] {'blk_1'}, dimensions={0}, use_global_device_ids=true | all-gather | bytes 491520 | tf_op jit(solution)/shard_map/all_gather | solution.py:21
  20.7 0.0 all-gather.2.cloned.1.call-update
  20.7 1.9 select_reduce_fusion
  22.7 0.7 broadcast_reduce_fusion
  23.4 0.9 select_reduce_fusion.1
  24.3 0.6 fusion.32
  26.2 2.9 broadcast_in_dim.21
  29.2 0.0 copy-done.2
  29.2 0.0 copy-done.1
  29.2 9.7 %all_gather.11 = bf16[512,256]{1,0:T(8,128)(2,1)S(1)} all-gather(bf16[128,256]{1,0:T(8,128)(2,1)S(1)} %pad_maximum_fusion.1), channel_id=1, replica_groups=mesh['head'=2,'blk_0'=8,'blk_1'=4,'rep'=4] {'rep'}, dimensions={0}, use_global_device_ids=true | all-gather | bytes 327680 | tf_op jit(solution)/shard_map/all_gather | solution.py:31
  38.9 30.7 %all-gather.2.cloned.1.call-done = bf16[4096,384]{0,1:T(8,128)(2,1)} async-done(((bf16[512,384]{0,1:T(8,128)(2,1)}), bf16[4096,384]{0,1:T(8,128)(2,1)}) %all-gather.2.cloned.1.call-update) | async-done | bytes 3145744 | tf_op jit(solution)/shard_map/all_gather | solution.py:21
  69.7 57.7 %conditional.1 = (f32[1,3,32,128,1]{3,0,4,1,2:T(1,128)S(1)}, f32[1,3,32,128,1]{3,0,4,1,2:T(1,128)S(1)}, f32[1,3,32,128,128]{3,0,4,1,2:T(1,128)}) conditional(s32[]{:T(128)} %convert_element_type.27, (f32[1,12288]{1,0:T(1,128)S(1)}, f32[1,12288]{1,0:T(1,128)S(1)}, f32[1,12288,128]{2,1,0:T(8,128)}) %tuple.35, (s32[512]{0:T(512)S(1)}, ...), branch_computations={%region_4.5_spmd, %region_5.8_spmd} | conditional | flops 3274727424 | bytes 111396888 | solution.py:108
  69.7 4.7 %copy.37 = bf16[1,3,4096,128]{3,2,1,0:T(8,128)(2,1)} copy(bf16[1,3,4096,128]{2,3,1,0:T(8,128)(2,1)} %get-tuple-element.124) | data formatting | bytes 6291456 | tf_op jit(solution)/shard_map
  74.4 12.3 %fusion.34 = (f32[12288]{0:T(1024)S(1)}, f32[12288,512]{0,1:T(8,128)}) fusion(bf16[12288,128]{1,0:T(8,128)(2,1)} %bitcast.54, bf16[512,256]{1,0:T(8,128)(2,1)S(1)} %get-tuple-element.84, s32[12288]{0:T(1024)S(1)} %le.16, s32[512]{0:T(512)S(1)} %get-tuple-element.81), kind=kOutput, calls=%fused_computation.61 | convolution fusion | flops 1635766272 | bytes 28542976 | tf_op jit(solution)/shard_map/while/body/eval_jaxpr/cond/branch_1_fun/hqd,khd->hqk/dot_general | solution.py:86
  86.7 0.1 max.2
  86.8 10.1 %fusion.1 = f32[12288]{0:T(1024)S(1)} fusion(f32[12288,512]{0,1:T(8,128)} %get-tuple-element.137, f32[12288]{0:T(1024)S(1)} %bitcast.57), kind=kLoop, calls=%fused_computation.3 | loop fusion | flops 12570624 | bytes 25264128 | tf_op jit(solution)/shard_map/while/body/eval_jaxpr/cond/branch_1_fun/reduce_sum | solution.py:96
  96.9 0.1 multiply_add_fusion
  97.0 15.6 %fusion.2 = f32[1,12288,128]{2,1,0:T(8,128)} fusion(f32[12288,512]{0,1:T(8,128)} %get-tuple-element.137, f32[12288]{0:T(1024)S(1)} %bitcast.58, f32[1,12288,128]{2,1,0:T(8,128)} %get-tuple-element.86, f32[12288]{0:T(1024)S(1)} %bitcast.63, bf16[512,256]{1,0:T(8,128)(2,1)S(1)} %get-tuple-element.84), kind=kOutput, calls=%fused_computation.5 | convolution fusion | flops 1626341376 | bytes 37978112 | tf_op jit(solution)/shard_map/while/body/eval_jaxpr/cond/branch_1_fun/hqk,khd->hqd/dot_general | solution.py:97
  112.6 14.6 %copy.53 = f32[1,3,32,128,128]{3,0,4,1,2:T(1,128)} copy(f32[1,3,32,128,128]{4,3,2,1,0:T(8,128)} %bitcast.52) | data formatting | bytes 12582912 | tf_op jit(solution)/shard_map/while/body/eval_jaxpr/cond
  127.2 0.1 copy.51
  127.3 0.1 copy.49
  127.4 6.9 %pad_maximum_fusion = f32[1,3,32,128,130]{3,0,4,1,2:T(1,128)S(1)} fusion(f32[1,3,32,128,128]{3,0,4,1,2:T(1,128)} %get-tuple-element.131, f32[1,3,32,128,1]{3,0,4,1,2:T(1,128)S(1)} %get-tuple-element.130, f32[1,3,32,128,1]{3,0,4,1,2:T(1,128)S(1)} %get-tuple-element.129), kind=kLoop, calls=%fused_computation.11 | loop fusion | flops 3194880 | bytes 12779520 | tf_op jit(solution)/shard_map/concatenate | solution.py:36
  134.2 150.0 %all_to_all.10 = f32[1,3,32,128,130]{3,0,4,1,2:T(1,128)S(1)} all-to-all(f32[1,3,32,128,130]{3,0,4,1,2:T(1,128)S(1)} %pad_maximum_fusion), channel_id=1, replica_groups=mesh['head'=2,'blk_0'=8,'blk_1'=4,'rep'=4] {'blk_0','blk_1'}, dimensions={2} | all-to-all | bytes 12779520 | tf_op jit(solution)/shard_map/all_to_all | solution.py:39
  284.2 0.1 slice_reduce_fusion
  284.4 0.6 log_add_fusion
  285.0 0.6 split.20
  285.6 4.3 %fusion.7 = f32[3,128,128]{1,0,2:T(4,128)S(1)} fusion(f32[1,3,32,128,128]{3,0,4,1,2:T(1,128)S(1)} %split.20, f32[3,32,128]{2,1,0:T(8,128)S(1)} %exponential_bitcast_fusion), kind=kLoop, calls=%fused_computation.13 | loop fusion | flops 3096576 | bytes 6537216 | tf_op jit(solution)/shard_map/reduce_sum | solution.py:166
  289.9 0.0 copy-done
  289.9 0.6 convolution_convert_fusion
  290.5 0.1 copy.70
  290.6 6.6 %all_to_all.11 = bf16[2,128,1536]{2,1,0:T(8,128)(2,1)S(1)} all-to-all(bf16[2,128,1536]{2,1,0:T(8,128)(2,1)S(1)} %bitcast.55), channel_id=1, replica_groups=mesh['head'=2,'blk_0'=8,'blk_1'=4,'rep'=4] {'head'}, dimensions={0} | all-to-all | bytes 1572864 | tf_op jit(solution)/shard_map/all_to_all | solution.py:54
  297.2 1.0 reduce_sum.67
  (12 shorter events, 0.3 us)
Async XLA Ops:
  7.2 282.7 %copy-start = (bf16[384,3072]{1,0:T(8,128)(2,1)S(1)}, bf16[384,3072]{1,0:T(8,128)(2,1)}, u32[]{:S(2)}) copy-start(bf16[384,3072]{1,0:T(8,128)(2,1)} %param.11) | copy-start | bytes 7077892
  7.2 22.0 %copy-start.2 = (bf16[128,128]{1,0:T(8,128)(2,1)S(1)}, bf16[128,128]{1,0:T(8,128)(2,1)}, u32[]{:S(2)}) copy-start(bf16[128,128]{1,0:T(8,128)(2,1)} %param.8) | copy-start | bytes 98308
  7.2 22.0 %copy-start.1 = (bf16[128,128]{1,0:T(8,128)(2,1)S(1)}, bf16[128,128]{1,0:T(8,128)(2,1)}, u32[]{:S(2)}) copy-start(bf16[128,128]{1,0:T(8,128)(2,1)} %param.9) | copy-start | bytes 98308
  7.2 62.5 %all-gather.2.cloned.1.call-start = ((), (), s32[]{:S(2)}) async-start(), calls=%async_computation.2 | async-start | bytes 3538944 | tf_op jit(solution)/shard_map/all_gather | solution.py:21
Sparse Core Ops, SparseCore 0:
  20.8 48.7 all-gather.1
where the time goes:
time: 306 us; the launch traced here: 305 us
  blocking collectives  179 us (58%)
  waiting for transfers between devices  30.7 us (10%)
  matrix products  28.5 us (9%)
  other arithmetic  27.3 us (9%)
  local copies, waits for them, and re-layouts  24.3 us (8%)
  between operations  15.5 us (5%)
    all_to_all x1, blocking collectives, side_by_side_2(): lax.all_to_all(both, axis, split_axis=split_dim, concat_axis=concat_dim,...  150 us
    all_gather x1, waiting for transfers between devices, whole_of(): x = lax.all_gather(x, axis, axis=dim, tiled=True)  30.7 us
    dot_general x1, matrix products, update(): jnp.einsum('hqk,khd->hqd', weights.astype(jnp.bfloat16), value_table, pre...  15.6 us
    cond x3, local copies, waits for them, and re-layouts  14.7 us
    dot_general x1, matrix products, update(): jnp.einsum('hqd,khd->hqk', query_heads, key_table, preferred_element_type...  12.3 us
    all_gather x1, blocking collectives, whole_of(): x = lax.all_gather(x, axis, axis=dim, tiled=True)  12.3 us
    reduce_sum x1, other arithmetic, update(): totals = totals * rescale + jnp.sum(weights, axis=2)  10.1 us
    all_gather x1, blocking collectives, side_by_side(): lax.all_gather(both, axis, axis=dim, tiled=True)  9.72 us
  transfers between devices with their start and end apart: 1, of which 1 were waited for; matrix products, arithmetic and copies ran while one was open for 2% of the time, Pallas kernels for 0%

commit v1 on v0

v1 whole, which is shorter than its diff:
```python
import functools
import heapq
import math

import jax
import jax.numpy as jnp
from jax import lax
from jax.experimental import pallas as pl
from jax.experimental.pallas import tpu as pltpu
from jax.sharding import Mesh
from jax.sharding import PartitionSpec as P

GROUP = 3
DH = 128
BLK_REP = ("blk_0", "blk_1", "rep")
AXIS = {"z": "blk_0", "x": "blk_1", "y": "rep"}
NEG = -1e30
LOG2E = 1.0 / math.log(2.0)
LN2 = math.log(2.0)
WHOLE, FIRST, SECOND = 0, 1, 2
SLOT_DY = (0, 1, 3, 2)


def ring_sends(offset, n):
    half, out = n // 2, []
    if offset == 0 or offset < half:
        new = offset + 1
        if new <= half:
            out.append((1, new, WHOLE if new < half else FIRST))
    if offset == 0 or offset > half:
        new = (offset or n) - 1
        if new >= half:
            out.append((-1, new, WHOLE if new > half else SECOND))
    return out


def parts_of(key, nz, nx, ny):
    if key[0] == "q":
        return 2 if key[1] == ny // 2 else 1
    _, half, dz, dx = key
    if half == 0:
        return 2 if (dz == 0 and dx == nx // 2) or dz == nz // 2 else 1
    return 2 if (dx == 0 and dz == nz // 2) or dx == nx // 2 else 1


def sends_of(key, nz, nx, ny):
    if key[0] == "q":
        return [("y", s, ("q", new), p) for s, new, p in ring_sends(key[1], ny)]
    _, half, dz, dx = key
    along_z = [("z", s, ("kv", half, new, dx), p) for s, new, p in ring_sends(dz, nz)]
    along_x = [("x", s, ("kv", half, dz, new), p) for s, new, p in ring_sends(dx, nx)]
    if half == 0:
        return (along_x if dz == 0 else []) + along_z
    return (along_z if dx == 0 else []) + along_x


def planes_in_order(nz):
    order = [0]
    for d in range(1, nz // 2):
        order += [d, nz - d]
    return order + [nz // 2]


def compute_units(nz, nx):
    planes = planes_in_order(nz)
    pieces = lambda p: [("kv", h, p, dx) for h in (0, 1) for dx in range(nx)]
    need_q = [[("q", SLOT_DY[0]), ("q", SLOT_DY[1])], [("q", SLOT_DY[2]), ("q", SLOT_DY[3])]]
    units = [(("first", r, 0), pieces(0) + need_q[r], 0.6) for r in (0, 1)]
    for c in range((nz - 2) // 2):
        needs = pieces(planes[1 + 2 * c]) + pieces(planes[2 + 2 * c])
        units += [(("main", r, c), needs + need_q[r], 1.0) for r in (0, 1)]
    units += [(("last", slot, 0), pieces(nz // 2), 0.35) for slot in (3, 1, 2, 0)]
    return units


def plan(nz, nx, ny, latency=2.0, rate=46500.0, issue=0.02):
    units = compute_units(nz, nx)
    busy, coming, took, done, steps, now = {}, [], {}, set(), [], 0.0

    def complete(key):
        done.add(key)
        size = 98304 if key[0] == "q" else 32768
        for axis, sign, new, part in sends_of(key, nz, nx, ny):
            nbytes = size if part == WHOLE else size // 2
            end = max(busy.get((axis, sign), 0.0), now) + nbytes / rate
            busy[axis, sign] = end
            heapq.heappush(coming, (end + latency, new, part))

    for key in (("kv", 0, 0, 0), ("kv", 1, 0, 0), ("q", 0)):
        complete(key)
    while coming or units:
        if coming and coming[0][0] <= now:
            _, key, part = heapq.heappop(coming)
            now += issue
            steps.append(("take", key, part))
            took[key] = took.get(key, 0) + 1
            if took[key] == parts_of(key, nz, nx, ny):
                complete(key)
            continue
        ready, seen = [], set()
        for u in units:
            rows = u[0][1] // 2 if u[0][0] == "last" else u[0][1]
            if rows not in seen and all(d in done for d in u[1]):
                ready.append(u)
            seen.add(rows)
        if ready:
            units.remove(ready[0])
            now += ready[0][2]
            steps.append(ready[0][0])
            continue
        now = coming[0][0]
    return steps


def kernel(
    sizes,
    q_hbm, k_hbm, v_hbm, order_ref, w_hbm,
    out_ref, lse_ref,
    q_buf, kv, m_buf, acc, w_buf, own_o, own_st, o_send, st_send, o_recv, st_recv, relay,
    p_send, p_recv,
    load_sem, kv_recv, q_recv, kv_send, q_send, o_send_sem, st_send_sem, o_recv_sem, st_recv_sem,
    relay_sem, relay_send, p_sem,
):
    nz, nx, ny = sizes
    tok = k_hbm.shape[0]
    hb = tok // 2
    head = lax.axis_index("head")
    pos = {a: lax.axis_index(AXIS[a]) for a in "zxy"}
    size = {"z": nz, "x": nx, "y": ny}

    def at(axis, delta):
        n = size[axis]
        return lax.rem(pos[axis] + (delta + n), n)

    def peer(axis, delta):
        return {AXIS[axis]: at(axis, delta)}

    loads = []
    for g in range(GROUP):
        loads.append((q_hbm.at[:, g * DH:(g + 1) * DH], q_buf.at[0, g]))
    for h in (0, 1):
        loads.append((k_hbm.at[h * hb:(h + 1) * hb], kv.at[0, h, 0]))
        loads.append((v_hbm.at[h * hb:(h + 1) * hb], kv.at[0, h, 1]))
    for c in (0, 1):
        width = out_ref.shape[1]
        loads.append((w_hbm.at[:, c * width:(c + 1) * width], w_buf.at[c]))
    loads = [pltpu.make_async_copy(s, d, load_sem.at[i]) for i, (s, d) in enumerate(loads)]
    for copy in loads[3:7] + loads[:3]:
        copy.start()

    barrier = pltpu.get_barrier_semaphore()
    peers = [peer(a, s) for a in "zxy" for s in (1, -1)] + [peer("y", 2), {"head": 1 - head}]
    for p in peers:
        pl.semaphore_signal(barrier, inc=1, device_id=p, device_id_type=pl.DeviceIdType.MESH)
    for copy in loads[3:7]:
        copy.wait()
    pl.semaphore_wait(barrier, len(peers))

    planes = planes_in_order(nz)
    place = {p: i for i, p in enumerate(planes)}

    def view(key, part):
        if key[0] == "q":
            ref = q_buf.at[SLOT_DY.index(key[1])]
            if part == WHOLE:
                return ref
            return ref.at[:, (part - 1) * hb:part * hb]
        _, h, dz, dx = key
        ref = kv.at[place[dz] * nx + dx, h]
        return ref if part == WHOLE else ref.at[part - 1]

    def arrival_sem(key, part):
        second = 1 if part == SECOND else 0
        if key[0] == "q":
            return q_recv.at[2 * key[1] + second]
        _, h, dz, dx = key
        return kv_recv.at[((h * nz + dz) * nx + dx) * 2 + second]

    def send_on(key):
        for axis, sign, new, part in sends_of(key, nz, nx, ny):
            pltpu.make_async_remote_copy(
                src_ref=view(key, part),
                dst_ref=view(new, part),
                send_sem=q_send if key[0] == "q" else kv_send,
                recv_sem=arrival_sem(new, part),
                device_id=peer(axis, sign),
                device_id_type=pl.DeviceIdType.MESH,
            ).start()

    taken = {}

    def take(key, part):
        ref = view(key, part)
        pltpu.make_async_copy(ref, ref, arrival_sem(key, part)).wait()
        taken[key] = taken.get(key, 0) + 1
        if taken[key] == parts_of(key, nz, nx, ny):
            send_on(key)

    factor = DH ** (-0.5) * LOG2E

    def query_place(slot):
        return order_ref[(pos["z"] * nx + pos["x"]) * ny + at("y", -SLOT_DY[slot])]

    def key_place(plane, dx):
        return order_ref[(at("z", -plane) * nx + at("x", -dx)) * ny + pos["y"]]

    def bias_row(slot, chunk):
        mine = query_place(slot)
        parts = []
        for plane in chunk:
            for dx in range(nx):
                b = jnp.where(key_place(plane, dx) > mine, NEG, 0.0).astype(jnp.float32)
                parts.append(jnp.full((1, tok), b, jnp.float32))
        return jnp.concatenate(parts, axis=1)

    def rows_of(which, chunk):
        rows = []
        for plane in chunk:
            for dx in range(nx):
                for h in (0, 1):
                    rows.append(kv[place[plane] * nx + dx, h, which])
        return jnp.concatenate(rows, axis=0)

    def attend(slots, chunk, first):
        key_rows = rows_of(0, chunk)
        value_rows = rows_of(1, chunk)
        value_rows = jnp.concatenate([value_rows, jnp.ones_like(value_rows)], axis=1)
        for slot in slots:
            bias = bias_row(slot, chunk)
            if first and slot == 0:
                r = lax.broadcasted_iota(jnp.int32, (tok, tok), 0)
                c = lax.broadcasted_iota(jnp.int32, (tok, tok), 1)
                corner = jnp.where(c <= r, 0.0, NEG).astype(jnp.float32)
                rest = jnp.broadcast_to(bias[:, tok:], (tok, bias.shape[1] - tok))
                bias = jnp.concatenate([corner, rest], axis=1)
            for g in range(GROUP):
                scores = lax.dot_general(
                    q_buf[slot, g], key_rows, (((1,), (1,)), ((), ())),
                    preferred_element_type=jnp.float32,
                )
                scores = scores * factor + bias
                top = jnp.max(scores, axis=1, keepdims=True)
                if not first:
                    old = m_buf[slot, g]
                    new = jnp.maximum(old, top)
                    shrink = jnp.exp2(old - new)
                    top = new[:, :1]
                else:
                    new = jnp.broadcast_to(top, (tok, DH))
                weights = jnp.exp2(scores - top).astype(jnp.bfloat16)
                both = jnp.dot(weights, value_rows, preferred_element_type=jnp.float32)
                if not first:
                    both = both + acc[slot, g] * jnp.concatenate([shrink, shrink], axis=1)
                m_buf[slot, g] = new
                acc[slot, g] = both

    def finish(slot):
        row = lax.broadcasted_iota(jnp.int32, (8, tok), 0)
        stats = None
        for g in range(GROUP):
            both = acc[slot, g]
            total = both[:, DH:]
            o = both[:, :DH] / total
            flat = jnp.transpose(m_buf[slot, g] + jnp.log(total) * LOG2E)[:8]
            stats = flat if g == 0 else jnp.where(row < g, stats, flat)
            if slot == 0:
                own_o[g] = o
            else:
                o_send[slot, g] = o.astype(jnp.bfloat16)
        if slot == 0:
            own_st[...] = stats
        else:
            st_send[slot] = stats

    def remote(src, dst, send, recv, to):
        return pltpu.make_async_remote_copy(
            src_ref=src, dst_ref=dst, send_sem=send, recv_sem=recv,
            device_id=to, device_id_type=pl.DeviceIdType.MESH,
        )

    def back(slot):
        dy = SLOT_DY[slot]
        st = remote(st_send.at[slot], st_recv.at[slot], st_send_sem.at[slot], st_recv_sem.at[slot],
                    peer("y", -dy if dy < ny - 1 else 1))
        if dy == ny // 2:
            return [
                remote(o_send.at[slot, :, :hb], relay.at[0], o_send_sem.at[0], relay_sem.at[0],
                       peer("y", 1)),
                remote(o_send.at[slot, :, hb:], relay.at[1], o_send_sem.at[3], relay_sem.at[1],
                       peer("y", -1)),
                st,
            ]
        return [
            remote(o_send.at[slot], o_recv.at[slot], o_send_sem.at[slot], o_recv_sem.at[slot],
                   peer("y", -1 if dy == 1 else 1)),
            st,
        ]

    send_on(("kv", 1, 0, 0))
    send_on(("kv", 0, 0, 0))
    for copy in loads[:3]:
        copy.wait()
    send_on(("q", 0))
    for copy in loads[7:]:
        copy.start()

    sent = []
    for step in plan(nz, nx, ny):
        if step[0] == "take":
            take(*step[1:])
            continue
        kind, which, c = step
        if kind == "first":
            attend((0, 1) if which == 0 else (2, 3), (0,), True)
        elif kind == "main":
            attend((0, 1) if which == 0 else (2, 3), planes[1 + 2 * c:3 + 2 * c], False)
        else:
            attend((which,), (nz // 2,), False)
            finish(which)
            if which:
                copies = back(which)
                for copy in copies:
                    copy.start()
                sent += copies

    far = SLOT_DY.index(ny // 2)
    onward = [
        remote(relay.at[0], o_recv.at[far, :, :hb], relay_send.at[0], o_recv_sem.at[0], peer("y", 1)),
        remote(relay.at[1], o_recv.at[far, :, hb:], relay_send.at[1], o_recv_sem.at[3], peer("y", -1)),
    ]
    for i, copy in enumerate(onward):
        pltpu.make_async_copy(relay.at[i], relay.at[i], relay_sem.at[i]).wait()
        copy.start()

    for copy in loads[7:]:
        copy.wait()
    for slot in (1, 2, 3):
        pltpu.make_async_copy(st_recv.at[slot], st_recv.at[slot], st_recv_sem.at[slot]).wait()
    logs = [own_st[...]] + [st_recv[slot] for slot in (1, 2, 3)]
    top = functools.reduce(jnp.maximum, logs)
    parts = [jnp.exp2(a - top) for a in logs]
    total = functools.reduce(jnp.add, parts)
    lse_ref[...] = (top * LN2 + jnp.log(total))[:GROUP]
    shares = [p / total for p in parts]
    shares = jnp.concatenate(shares + [jnp.zeros((DH - 32, tok), jnp.float32)], axis=0)
    shares = jnp.transpose(shares)

    for slot in (1, 2):
        pltpu.make_async_copy(o_recv.at[slot], o_recv.at[slot], o_recv_sem.at[slot]).wait()
    for copy in onward:
        copy.wait_recv()
    attended = []
    for g in range(GROUP):
        o = own_o[g] * shares[:, g:g + 1]
        for slot in (1, 2, 3):
            o = o + o_recv[slot, g].astype(jnp.float32) * shares[:, 8 * slot + g:8 * slot + g + 1]
        attended.append(o.astype(jnp.bfloat16))
    attended = jnp.concatenate(attended, axis=1)

    width = out_ref.shape[1]
    tile = width // 3
    for j in range(0, width, tile):
        p = jnp.dot(attended, w_buf[1 - head, :, j:j + tile], preferred_element_type=jnp.float32)
        p_send[:, j:j + tile] = p.astype(jnp.bfloat16)
    swap = remote(p_send, p_recv, p_sem.at[0], p_sem.at[1], {"head": 1 - head})
    swap.start()
    for j in range(0, width, tile):
        p = jnp.dot(attended, w_buf[head, :, j:j + tile], preferred_element_type=jnp.float32)
        out_ref[:, j:j + tile] = p.astype(jnp.bfloat16)
    swap.wait_recv()
    out_ref[...] = (out_ref[...].astype(jnp.float32) + p_recv[...].astype(jnp.float32)).astype(
        jnp.bfloat16
    )

    pltpu.make_async_copy(kv.at[1:], kv.at[1:], kv_send).wait()
    pltpu.make_async_copy(q_buf.at[1:], q_buf.at[1:], q_send).wait()
    for copy in sent + onward + [swap]:
        copy.wait_send()


def body(sizes, queries, keys, values, stretch_order, out_weight):
    nz, nx, ny = sizes
    tok = queries.shape[0]
    width = out_weight.shape[1] // 2
    bf, f32 = jnp.bfloat16, jnp.float32
    hbm = pl.BlockSpec(memory_space=pl.ANY)
    dma = pltpu.SemaphoreType.DMA
    call = pl.pallas_call(
        functools.partial(kernel, sizes),
        name="attend_and_project",
        out_shape=(
            jax.ShapeDtypeStruct((tok, width), bf),
            jax.ShapeDtypeStruct((GROUP, tok), f32),
        ),
        in_specs=[hbm, hbm, hbm, pl.BlockSpec(memory_space=pltpu.SMEM), hbm],
        out_specs=(
            pl.BlockSpec(memory_space=pltpu.VMEM),
            pl.BlockSpec(memory_space=pltpu.VMEM),
        ),
        scratch_shapes=[
            pltpu.VMEM((ny, GROUP, tok, DH), bf),
            pltpu.VMEM((nz * nx, 2, 2, tok // 2, DH), bf),
            pltpu.VMEM((ny, GROUP, tok, DH), f32),
            pltpu.VMEM((ny, GROUP, tok, 2 * DH), f32),
            pltpu.VMEM((2, GROUP * DH, width), bf),
            pltpu.VMEM((GROUP, tok, DH), f32),
            pltpu.VMEM((8, tok), f32),
            pltpu.VMEM((ny, GROUP, tok, DH), bf),
            pltpu.VMEM((ny, 8, tok), f32),
            pltpu.VMEM((ny, GROUP, tok, DH), bf),
            pltpu.VMEM((ny, 8, tok), f32),
            pltpu.VMEM((2, GROUP, tok // 2, DH), bf),
            pltpu.VMEM((tok, width), bf),
            pltpu.VMEM((tok, width), bf),
            dma((9,)),
            dma((4 * nz * nx,)),
            dma((2 * ny,)),
            dma,
            dma,
            dma((4,)),
            dma((4,)),
            dma((4,)),
            dma((4,)),
            dma((2,)),
            dma((2,)),
            dma((2,)),
        ],
        compiler_params=pltpu.CompilerParams(
            collective_id=0, has_side_effects=True, vmem_limit_bytes=60 * 1024 * 1024
        ),
    )
    return call(queries, keys, values, stretch_order, out_weight)


def solution(mesh):
    nz, nx, ny = 8, 4, mesh.shape["rep"]
    split = Mesh(
        mesh.devices.reshape(mesh.shape["head"], nz, nx, ny),
        ("head", "blk_0", "blk_1", "rep"),
    )
    in_specs = (P(BLK_REP, "head"), P(BLK_REP, "head"), P(BLK_REP, "head"), P(), P("head", None))
    out_specs = (P(BLK_REP, "head"), P("head", BLK_REP))
    return jax.shard_map(
        functools.partial(body, (nz, nx, ny)),
        mesh=split, in_specs=in_specs, out_specs=out_specs, check_vma=False,
    )
```

time: 306 us -> 51.8 us (0.17)
  blocking collectives: 179 us -> 0 us
  Pallas kernels: 0 us -> 48 us
  waiting for transfers between devices: 30.7 us -> 0 us
  matrix products: 28.5 us -> 0 us
  other arithmetic: 27.3 us -> 0 us
  local copies, waits for them, and re-layouts: 24.3 us -> 3 us
  between operations: 15.5 us -> 0.64 us
    all_to_all x2 -> x0, blocking collectives: 157 us -> none  [the longest x1 150 us: side_by_side_2(): lax.all_to_all(both, axis, split_axis=split_dim, concat_axis=concat_dim,...]
    pallas_call x0 -> x1, Pallas kernels: none -> 48 us  [body(): return call(queries, keys, values, stretch_order, out_weight)]
    all_gather x1 -> x0, waiting for transfers between devices: 30.7 us -> none  [whole_of(): x = lax.all_gather(x, axis, axis=dim, tiled=True)]
    dot_general x3 -> x0, matrix products: 28.5 us -> none  [the longest x1 15.6 us: update(): jnp.einsum('hqk,khd->hqd', weights.astype(jnp.bfloat16), value_table, pre...]
    all_gather x2 -> x0, blocking collectives: 22 us -> none  [the longest x1 12.3 us: whole_of(): x = lax.all_gather(x, axis, axis=dim, tiled=True)]
    reduce_sum x6 -> x0, other arithmetic: 18.2 us -> none  [the longest x1 10.1 us: update(): totals = totals * rescale + jnp.sum(weights, axis=2)]
    cond x3 -> x0, local copies, waits for them, and re-layouts: 14.7 us -> none
    concatenate x2 -> x0, other arithmetic: 6.87 us -> none  [the longest x1 6.86 us: side_by_side_2(): jnp.concatenate([a.reshape(*a.shape[:along], w) for a, w in zip(arrays, w...]
  transfers between devices with their start and end apart: 1 -> 0, of which waited for: 1 -> 0; matrix products, arithmetic and copies ran while one was open for 2% -> 0% of each run, Pallas kernels for 0% -> 0%
where the time goes in v1:
time: 51.8 us; the launch traced here: 51.6 us
  Pallas kernels  48 us (93%)
  local copies, waits for them, and re-layouts  3 us (6%)
  between operations  0.64 us (1%)
    pallas_call x1, Pallas kernels, body(): return call(queries, keys, values, stretch_order, out_weight)  48 us
    unnamed x2, local copies, waits for them, and re-layouts  3 us

profile of v1, /device:TPU:1, one launch (start us, length us, event | category | flops | bytes accessed | tf_op | source)
XLA Modules:
  0.0 51.6 jit_solution(1605648879480383813)
XLA Ops:
  0.6 48.0 %attend_and_project.1 = (bf16[128,1536]{1,0:T(8,128)(2,1)}, f32[3,128]{1,0:T(4,128)}) custom-call(bf16[128,384]{1,0:T(8,128)(2,1)} %q_hbm.1, bf16[128,128]{1,0:T(8,128)(2,1)} %k_hbm.1, bf16[128,128]{1,0:T(8,128)(2,1)} %v_hbm.1, s32[128]{0:T(128)} %order_ref.1, bf16[384,3072]{1,0:T(8,128)(2,1)} %w_hbm.1), custom_call_target="tpu_custom_call" | custom-call | tf_op jit(solution)/shard_map/attend_and_project/pallas_call | solution.py:432
  48.6 1.8 %copy.9 = bf16[128,1536]{1,0:T(8,128)(2,1)} copy(bf16[128,1536]{1,0:T(8,128)(2,1)} %get-tuple-element.4) | data formatting | bytes 786432
  50.4 1.2 %copy.10 = f32[3,128]{1,0:T(4,128)} copy(f32[3,128]{1,0:T(4,128)} %get-tuple-element.5) | data formatting | bytes 3072

commit v2 on v1

v2 whole, which is shorter than its diff:
```python
import functools
import heapq
import math

import jax
import jax.numpy as jnp
from jax import lax
from jax.experimental import pallas as pl
from jax.experimental.pallas import tpu as pltpu
from jax.sharding import Mesh
from jax.sharding import PartitionSpec as P

GROUP = 3
DH = 128
BLK_REP = ("blk_0", "blk_1", "rep")
AXIS = {"z": "blk_0", "x": "blk_1", "y": "rep"}
NEG = -1e30
LOG2E = 1.0 / math.log(2.0)
LN2 = math.log(2.0)
WHOLE, FIRST, SECOND = 0, 1, 2
SLOT_DY = (0, 1, 3, 2)


RELAY, DIRECT, STRIDE = 0, 1, 2


def ring_sends(mode, offset, n):
    half = n // 2
    if mode == DIRECT:
        if offset:
            return []
        near = [(s * k, s * k % n, WHOLE) for k in range(1, half) for s in (1, -1)]
        return near + [(half, half, WHOLE)]
    if mode == STRIDE and n == 8:
        if offset == 0:
            return [(1, 1, WHOLE), (-1, 7, WHOLE), (2, 2, WHOLE), (-2, 6, WHOLE)]
        if offset == 2:
            return [(1, 3, WHOLE), (2, 4, FIRST)]
        if offset == 6:
            return [(-1, 5, WHOLE), (-2, 4, SECOND)]
        return []
    out = []
    if offset == 0 or offset < half:
        new = offset + 1
        if new <= half:
            out.append((1, new, WHOLE if new < half else FIRST))
    if offset == 0 or offset > half:
        new = (offset or n) - 1
        if new >= half:
            out.append((-1, new, WHOLE if new > half else SECOND))
    return out


def parts_in(mode, offset, n):
    return 2 if mode != DIRECT and offset == n // 2 else 1


X_FIRST, Z_SECOND, Z_FIRST, X_SECOND, Q_RING = DIRECT, RELAY, STRIDE, RELAY, DIRECT


def parts_of(key, nz, nx, ny):
    if key[0] == "q":
        return parts_in(Q_RING, key[1], ny)
    _, half, dz, dx = key
    if half == 0:
        return parts_in(X_FIRST, dx, nx) if dz == 0 else parts_in(Z_SECOND, dz, nz)
    return parts_in(Z_FIRST, dz, nz) if dx == 0 else parts_in(X_SECOND, dx, nx)


def sends_of(key, nz, nx, ny):
    if key[0] == "q":
        return [("y", s, ("q", new), p) for s, new, p in ring_sends(Q_RING, key[1], ny)]
    _, half, dz, dx = key
    modes = (X_FIRST, Z_SECOND) if half == 0 else (X_SECOND, Z_FIRST)
    along_x = [("x", s, ("kv", half, dz, new), p) for s, new, p in ring_sends(modes[0], dx, nx)]
    along_z = [("z", s, ("kv", half, new, dx), p) for s, new, p in ring_sends(modes[1], dz, nz)]
    if half == 0:
        return (along_x if dz == 0 else []) + along_z
    return (along_z if dx == 0 else []) + along_x


def planes_in_order(nz):
    order = [0]
    for d in range(1, nz // 2):
        order += [d, nz - d]
    return order + [nz // 2]


def compute_units(nz, nx):
    planes = planes_in_order(nz)
    pieces = lambda p: [("kv", h, p, dx) for h in (0, 1) for dx in range(nx)]
    need_q = [[("q", SLOT_DY[0]), ("q", SLOT_DY[1])], [("q", SLOT_DY[2]), ("q", SLOT_DY[3])]]
    units = [(("first", r, 0), pieces(0) + need_q[r], 0.5) for r in (0, 1)]
    for c in range((nz - 2) // 2):
        needs = pieces(planes[1 + 2 * c]) + pieces(planes[2 + 2 * c])
        units += [(("main", r, c), needs + need_q[r], 0.85) for r in (0, 1)]
    units += [(("last", slot, 0), pieces(nz // 2), 0.3) for slot in (3, 1, 2, 0)]
    return units


def plan(nz, nx, ny, latency=2.3, hop=0.75, rate=50000.0, issue=0.03):
    units = compute_units(nz, nx)
    busy, coming, took, done, steps, now = {}, [], {}, set(), [], 0.0
    counts = {"z": nz, "x": nx, "y": ny}

    def complete(key):
        done.add(key)
        size = 98304 if key[0] == "q" else (24576, 40960)[key[1]]
        for axis, step, new, part in sends_of(key, nz, nx, ny):
            time = (size if part == WHOLE else size // 2) / rate
            ways = (1, -1) if 2 * abs(step) == counts[axis] else (1 if step > 0 else -1,)
            end = 0.0
            for way in ways:
                busy[axis, way] = max(busy.get((axis, way), 0.0), now) + time * abs(step) / len(ways)
                end = max(end, busy[axis, way])
            heapq.heappush(coming, (end + latency + hop * (abs(step) - 1), new, part))

    for key in (("kv", 1, 0, 0), ("kv", 0, 0, 0), ("q", 0)):
        complete(key)
    while coming or units:
        if coming and coming[0][0] <= now:
            _, key, part = heapq.heappop(coming)
            now += issue
            steps.append(("take", key, part))
            took[key] = took.get(key, 0) + 1
            if took[key] == parts_of(key, nz, nx, ny):
                complete(key)
            continue
        ready, seen = [], set()
        for u in units:
            rows = u[0][1] // 2 if u[0][0] == "last" else u[0][1]
            if rows not in seen and all(d in done for d in u[1]):
                ready.append(u)
            seen.add(rows)
        if ready:
            units.remove(ready[0])
            now += ready[0][2]
            steps.append(ready[0][0])
            continue
        now = coming[0][0]
    return steps


def reached(nz, nx, ny):
    keys = [("kv", h, z, x) for h in (0, 1) for z in range(nz) for x in range(nx)]
    counts = {"z": nz, "x": nx, "y": ny}
    steps = {("y", k) for k in range(1, ny)}
    for key in keys + [("q", 0)]:
        for axis, step, _, _ in sends_of(key, nz, nx, ny):
            steps |= {(axis, step % counts[axis]), (axis, -step % counts[axis])}
    return sorted(steps)


def kernel(
    sizes,
    q_hbm, k_hbm, v_hbm, order_hbm, w_hbm,
    out_ref, lse_ref,
    order_ref, q_buf, kv, m_buf, acc, w_buf, w_other, own_o, own_st, o_send, st_send, o_recv, st_recv,
    att, att_recv,
    load_sem, kv_recv, q_recv, kv_send, q_send, o_send_sem, st_send_sem, o_recv_sem, st_recv_sem,
    swap_sem,
):
    nz, nx, ny = sizes
    tok = k_hbm.shape[0]
    cut = tok * 3 // 8
    width = out_ref.shape[1]
    head = lax.axis_index("head")
    pos = {a: lax.axis_index(AXIS[a]) for a in "zxy"}
    size = {"z": nz, "x": nx, "y": ny}

    def at(axis, delta):
        n = size[axis]
        return lax.rem(pos[axis] + (delta % n), n)

    def peer(axis, delta):
        return {AXIS[axis]: at(axis, delta)}

    def remote(src, dst, send, recv, to):
        return pltpu.make_async_remote_copy(
            src_ref=src, dst_ref=dst, send_sem=send, recv_sem=recv,
            device_id=to, device_id_type=pl.DeviceIdType.MESH,
        )

    loads = [(k_hbm, kv.at[0, 0]), (v_hbm, kv.at[0, 1])]
    for g in range(GROUP):
        loads.append((q_hbm.at[:, g * DH:(g + 1) * DH], q_buf.at[0, g]))
    loads.append((order_hbm, order_ref))
    for c in (0, 1):
        loads.append((w_hbm.at[:, c * width:(c + 1) * width], w_buf.at[c]))
    loads = [pltpu.make_async_copy(s, d, load_sem.at[i]) for i, (s, d) in enumerate(loads)]
    kv_loads, q_loads, w_loads = loads[:2], loads[2:6], loads[6:]
    for copy in kv_loads + q_loads:
        copy.start()

    barrier = pltpu.get_barrier_semaphore()
    partner = {"head": 1 - head}
    peers = [peer(*step) for step in reached(nz, nx, ny)] + [partner]
    for p in peers:
        pl.semaphore_signal(barrier, inc=1, device_id=p, device_id_type=pl.DeviceIdType.MESH)
    for copy in kv_loads:
        copy.wait()
    pl.semaphore_wait(barrier, len(peers))

    planes = planes_in_order(nz)
    place = {p: i for i, p in enumerate(planes)}

    def view(key, part):
        if key[0] == "q":
            return q_buf.at[SLOT_DY.index(key[1])]
        _, h, dz, dx = key
        rows = slice(0, cut) if h == 0 else slice(cut, tok)
        slot = place[dz] * nx + dx
        return kv.at[slot, :, rows] if part == WHOLE else kv.at[slot, part - 1, rows]

    def arrival_sem(key, part):
        if key[0] == "q":
            return q_recv.at[key[1]]
        _, h, dz, dx = key
        return kv_recv.at[((h * nz + dz) * nx + dx) * 2 + (1 if part == SECOND else 0)]

    def send_on(key):
        for axis, step, new, part in sends_of(key, nz, nx, ny):
            remote(
                view(key, part), view(new, part), q_send if key[0] == "q" else kv_send,
                arrival_sem(new, part), peer(axis, step),
            ).start()

    taken = {}

    def take(key, part):
        ref = view(key, part)
        pltpu.make_async_copy(ref, ref, arrival_sem(key, part)).wait()
        taken[key] = taken.get(key, 0) + 1
        if taken[key] == parts_of(key, nz, nx, ny):
            send_on(key)

    factor = DH ** (-0.5) * LOG2E

    def query_place(slot):
        return order_ref[(pos["z"] * nx + pos["x"]) * ny + at("y", -SLOT_DY[slot])]

    def key_place(plane, dx):
        return order_ref[(at("z", -plane) * nx + at("x", -dx)) * ny + pos["y"]]

    def bias_row(slot, chunk):
        mine = query_place(slot)
        parts = []
        for plane in chunk:
            for dx in range(nx):
                b = jnp.where(key_place(plane, dx) > mine, NEG, 0.0).astype(jnp.float32)
                parts.append(jnp.full((1, tok), b, jnp.float32))
        return jnp.concatenate(parts, axis=1)

    def rows_of(which, chunk):
        first = place[chunk[0]] * nx
        count = len(chunk) * nx
        return kv[first:first + count, which].reshape(count * tok, DH)

    def attend(slots, chunk, first):
        key_rows = rows_of(0, chunk)
        value_rows = rows_of(1, chunk)
        value_rows = jnp.concatenate([value_rows, jnp.ones_like(value_rows)], axis=1)
        for slot in slots:
            bias = bias_row(slot, chunk)
            if first and slot == 0:
                r = lax.broadcasted_iota(jnp.int32, (tok, tok), 0)
                c = lax.broadcasted_iota(jnp.int32, (tok, tok), 1)
                corner = jnp.where(c <= r, 0.0, NEG).astype(jnp.float32)
                rest = jnp.broadcast_to(bias[:, tok:], (tok, bias.shape[1] - tok))
                bias = jnp.concatenate([corner, rest], axis=1)
            for g in range(GROUP):
                scores = lax.dot_general(
                    q_buf[slot, g], key_rows, (((1,), (1,)), ((), ())),
                    preferred_element_type=jnp.float32,
                )
                scores = scores * factor + bias
                top = jnp.max(scores, axis=1, keepdims=True)
                if not first:
                    old = m_buf[slot, g]
                    new = jnp.maximum(old, top)
                    shrink = jnp.exp2(old - new)
                    top = new[:, :1]
                else:
                    new = jnp.broadcast_to(top, (tok, DH))
                weights = jnp.exp2(scores - top).astype(jnp.bfloat16)
                both = jnp.dot(weights, value_rows, preferred_element_type=jnp.float32)
                if not first:
                    both = both + acc[slot, g] * jnp.concatenate([shrink, shrink], axis=1)
                m_buf[slot, g] = new
                acc[slot, g] = both

    def finish(slot):
        row = lax.broadcasted_iota(jnp.int32, (8, tok), 0)
        stats = None
        for g in range(GROUP):
            both = acc[slot, g]
            total = both[:, DH:]
            o = both[:, :DH] / total
            flat = jnp.transpose(m_buf[slot, g] + jnp.log(total) * LOG2E)[:8]
            stats = flat if g == 0 else jnp.where(row < g, stats, flat)
            if slot == 0:
                own_o[g] = o
            else:
                o_send[slot, g] = o.astype(jnp.bfloat16)
        if slot == 0:
            own_st[...] = stats
        else:
            st_send[slot] = stats

    def back(slot):
        to = peer("y", -SLOT_DY[slot])
        return [
            remote(o_send.at[slot], o_recv.at[slot], o_send_sem.at[slot], o_recv_sem.at[slot], to),
            remote(st_send.at[slot], st_recv.at[slot], st_send_sem.at[slot], st_recv_sem.at[slot], to),
        ]

    send_on(("kv", 1, 0, 0))
    send_on(("kv", 0, 0, 0))
    for copy in q_loads:
        copy.wait()
    send_on(("q", 0))
    for copy in w_loads:
        copy.start()
    w_swap = remote(w_buf.at[1 - head], w_other, swap_sem.at[0], swap_sem.at[1], partner)

    sent = [w_swap]
    for step in plan(nz, nx, ny):
        if step[0] == "take":
            take(*step[1:])
            continue
        kind, which, c = step
        if kind == "first":
            attend((0, 1) if which == 0 else (2, 3), (0,), True)
            if which == 1:
                for copy in w_loads:
                    copy.wait()
                w_swap.start()
        elif kind == "main":
            attend((0, 1) if which == 0 else (2, 3), planes[1 + 2 * c:3 + 2 * c], False)
        else:
            attend((which,), (nz // 2,), False)
            finish(which)
            if which:
                copies = back(which)
                for copy in copies:
                    copy.start()
                sent += copies

    for slot in (1, 2, 3):
        pltpu.make_async_copy(st_recv.at[slot], st_recv.at[slot], st_recv_sem.at[slot]).wait()
    logs = [own_st[...]] + [st_recv[slot] for slot in (1, 2, 3)]
    top = functools.reduce(jnp.maximum, logs)
    parts = [jnp.exp2(a - top) for a in logs]
    total = functools.reduce(jnp.add, parts)
    lse_ref[...] = (top * LN2 + jnp.log(total))[:GROUP]
    shares = [p / total for p in parts]
    shares = jnp.concatenate(shares + [jnp.zeros((DH - 32, tok), jnp.float32)], axis=0)
    shares = jnp.transpose(shares)

    for slot in (1, 2, 3):
        pltpu.make_async_copy(o_recv.at[slot], o_recv.at[slot], o_recv_sem.at[slot]).wait()
    for g in range(GROUP):
        o = own_o[g] * shares[:, g:g + 1]
        for slot in (1, 2, 3):
            o = o + o_recv[slot, g].astype(jnp.float32) * shares[:, 8 * slot + g:8 * slot + g + 1]
        att[:, g * DH:(g + 1) * DH] = o.astype(jnp.bfloat16)
    swap = remote(att, att_recv, swap_sem.at[2], swap_sem.at[3], partner)
    swap.start()
    sent.append(swap)

    tile = width // 3
    attended = att[...]
    for j in range(0, width, tile):
        p = jnp.dot(attended, w_buf[head, :, j:j + tile], preferred_element_type=jnp.float32)
        out_ref[:, j:j + tile] = p.astype(jnp.bfloat16)
    w_swap.wait_recv()
    swap.wait_recv()
    attended = att_recv[...]
    for j in range(0, width, tile):
        p = jnp.dot(attended, w_other[:, j:j + tile], preferred_element_type=jnp.float32)
        p = p.astype(jnp.bfloat16).astype(jnp.float32)
        both = out_ref[:, j:j + tile].astype(jnp.float32) + p
        out_ref[:, j:j + tile] = both.astype(jnp.bfloat16)

    pltpu.make_async_copy(kv.at[1:], kv.at[1:], kv_send).wait()
    pltpu.make_async_copy(q_buf.at[1:], q_buf.at[1:], q_send).wait()
    for copy in sent:
        copy.wait_send()


def put_out(a_ref, b_ref, out_ref, lse_ref, sems):
    copies = [
        pltpu.make_async_copy(a_ref, out_ref, sems.at[0]),
        pltpu.make_async_copy(b_ref, lse_ref, sems.at[1]),
    ]
    for copy in copies:
        copy.start()
    for copy in copies:
        copy.wait()


def body(sizes, queries, keys, values, stretch_order, out_weight):
    nz, nx, ny = sizes
    tok = queries.shape[0]
    width = out_weight.shape[1] // 2
    bf, f32 = jnp.bfloat16, jnp.float32
    vmem = pl.BlockSpec(memory_space=pltpu.VMEM)
    hbm = pl.BlockSpec(memory_space=pltpu.HBM)
    dma = pltpu.SemaphoreType.DMA
    results = (
        jax.ShapeDtypeStruct((tok, width), bf),
        jax.ShapeDtypeStruct((GROUP, tok), f32),
    )
    call = pl.pallas_call(
        functools.partial(kernel, sizes),
        name="attend_and_project",
        out_shape=results,
        in_specs=[hbm] * 5,
        out_specs=(vmem, vmem),
        scratch_shapes=[
            pltpu.SMEM(stretch_order.shape, jnp.int32),
            pltpu.VMEM((ny, GROUP, tok, DH), bf),
            pltpu.VMEM((nz * nx, 2, tok, DH), bf),
            pltpu.VMEM((ny, GROUP, tok, DH), f32),
            pltpu.VMEM((ny, GROUP, tok, 2 * DH), f32),
            pltpu.VMEM((2, GROUP * DH, width), bf),
            pltpu.VMEM((GROUP * DH, width), bf),
            pltpu.VMEM((GROUP, tok, DH), f32),
            pltpu.VMEM((8, tok), f32),
            pltpu.VMEM((ny, GROUP, tok, DH), bf),
            pltpu.VMEM((ny, 8, tok), f32),
            pltpu.VMEM((ny, GROUP, tok, DH), bf),
            pltpu.VMEM((ny, 8, tok), f32),
            pltpu.VMEM((tok, GROUP * DH), bf),
            pltpu.VMEM((tok, GROUP * DH), bf),
            dma((8,)),
            dma((4 * nz * nx,)),
            dma((ny,)),
            dma,
            dma,
            dma((ny,)),
            dma((ny,)),
            dma((ny,)),
            dma((ny,)),
            dma((4,)),
        ],
        compiler_params=pltpu.CompilerParams(
            collective_id=0, has_side_effects=True, vmem_limit_bytes=32 * 1024 * 1024
        ),
    )
    args = (queries, keys, values, stretch_order, out_weight)
    mixed, logs = call(*(in_hbm(a) for a in args))
    return pl.pallas_call(
        put_out,
        name="put_out",
        out_shape=results,
        in_specs=[vmem, vmem],
        out_specs=(hbm, hbm),
        scratch_shapes=[dma((2,))],
        compiler_params=pltpu.CompilerParams(vmem_limit_bytes=4 * 1024 * 1024),
    )(mixed, logs)


def in_hbm(x):
    return pltpu.with_memory_space_constraint(x, pltpu.HBM)


def solution(mesh):
    nz, nx, ny = 8, 4, mesh.shape["rep"]
    split = Mesh(
        mesh.devices.reshape(mesh.shape["head"], nz, nx, ny),
        ("head", "blk_0", "blk_1", "rep"),
    )
    in_specs = (P(BLK_REP, "head"), P(BLK_REP, "head"), P(BLK_REP, "head"), P(), P("head", None))
    out_specs = (P(BLK_REP, "head"), P("head", BLK_REP))
    return jax.shard_map(
        functools.partial(body, (nz, nx, ny)),
        mesh=split, in_specs=in_specs, out_specs=out_specs, check_vma=False,
    )
```

time: 51.8 us -> 44.2 us (0.85)
  Pallas kernels: 48 us -> 43.4 us
  local copies, waits for them, and re-layouts: 3 us -> 0 us
    pallas_call x1 -> x2, Pallas kernels: 48 us -> 43.4 us  [the longest x1 42.6 us: body(): mixed, logs = call(*(in_hbm(a) for a in args))]
    unnamed x2 -> x0, local copies, waits for them, and re-layouts: 3 us -> none
where the time goes in v2:
time: 44.2 us; the launch traced here: 44 us
  Pallas kernels  43.4 us (98%)
  between operations  0.64 us (1%)
    pallas_call x1, Pallas kernels, body(): mixed, logs = call(*(in_hbm(a) for a in args))  42.6 us

profile of v2, /device:TPU:1, one launch (start us, length us, event | category | flops | bytes accessed | tf_op | source)
XLA Modules:
  0.0 44.0 jit_solution(144743825765558224)
XLA Ops:
  0.6 42.6 %attend_and_project.1 = (bf16[128,1536]{1,0:T(8,128)(2,1)S(1)}, f32[3,128]{1,0:T(4,128)S(1)}) custom-call(bf16[128,384]{1,0:T(8,128)(2,1)} %q_hbm.1, bf16[128,128]{1,0:T(8,128)(2,1)} %k_hbm.1, bf16[128,128]{1,0:T(8,128)(2,1)} %v_hbm.1, s32[128]{0:T(128)} %order_hbm.1, bf16[384,3072]{1,0:T(8,128)(2,1)} %w_hbm.1), custom_call_target="tpu_custom_call" | custom-call | tf_op jit(solution)/shard_map/attend_and_project/pallas_call | solution.py:452
  43.3 0.8 %put_out.1 = (bf16[128,1536]{1,0:T(8,128)(2,1)}, f32[3,128]{1,0:T(4,128)}) custom-call(bf16[128,1536]{1,0:T(8,128)(2,1)S(1)} %get-tuple-element.4.a_ref, f32[3,128]{1,0:T(4,128)S(1)} %get-tuple-element.5.b_ref), custom_call_target="tpu_custom_call" | custom-call | tf_op jit(solution)/shard_map/put_out/pallas_call | solution.py:453
